TPU v7x, 128 devices: a whole 4x4x4 slice. The times are simulated.
128 devices in a mesh: io: 16 (over z, y), cmp: 8 (over x, core).
Axes of the slice: x: 4, y: 4, z: 4, core: 2. Of those that a mesh axis runs over, the one named last changes fastest.
Arguments:
- fields: float32 [6, 8, 1024, 4096], P(None, None, 'cmp', 'io'), may hold values from -6 to 6
- mean_old: float32 [6, 8, 1024, 3072], P(None, 'cmp', 'io'), may hold values from -6 to 6
- land_mask: int32 [8, 1024, 4096], P('cmp', 'io'), may hold values from 0 to 1, as said below
Outputs:
- mean_new: float32 [6, 8, 1024, 3072], P(None, 'cmp', 'io')
- level_rms: float32 [6, 8], P(None, 'cmp')
Inputs may be any that keep to these rules, and one draw needn't show every extreme that they name: `land_mask`: each row (level, latitude) has between 1 and 3072 ocean points, and some row has exactly 3072.
All inputs are finite; a program needn't handle non-finite values.
Results may differ from a plain program's by a relative error of at most 0.00002.
Values sent between devices are 32-bit elements; how exact they have to be, the bound alone decides.
A program may use at most 128 MiB of HBM per device.

v0:
```python
import jax
import jax.numpy as jnp
from jax import lax
from jax.experimental import pallas as pl
from jax.experimental.pallas import tpu as pltpu
from jax.sharding import PartitionSpec as P

STEPS = 3
MESH = pl.DeviceIdType.MESH

FIELDS = 6
LON = 16
ROWS = 64
COLS = 256
CHUNKS = 32
OUT_CHUNKS = 24
PIECES = 2
PIECE_ROWS = ROWS // PIECES
GROUPS = ROWS // 8
PIECE_GROUPS = PIECE_ROWS // 8
ORDER = [(dx, dy, dc) for dy in (0, 1) for dc in (0, 1) for dx in (1, 3, 2, 0)]


def lanes_of(array, index):
    return jnp.take_along_axis(array, index, axis=1, mode="promise_in_bounds")


def plan_group(g, mask, place, arrive, count):
    rows = pl.ds(pl.multiple_of(g * 8, 8), 8)
    chunk = [mask[rows, pl.ds(c * 128, 128)] for c in range(CHUNKS)]
    stacked = jnp.concatenate(chunk, axis=0).astype(jnp.float32).astype(jnp.bfloat16)
    source = lax.broadcasted_iota(jnp.int32, (128, 256), 0)
    target = lax.broadcasted_iota(jnp.int32, (128, 256), 1)
    upto = ((source <= target) | (target >= 128)).astype(jnp.float32).astype(jnp.bfloat16)
    sums = jnp.dot(stacked, upto, preferred_element_type=jnp.float32).astype(jnp.int32)
    lane = lax.broadcasted_iota(jnp.int32, (8, 128), 1)
    base = jnp.zeros((8, 128), jnp.int32)
    state = []
    for c in range(CHUNKS):
        upto_here = sums[c * 8 : c * 8 + 8, :128]
        number = sums[c * 8 : c * 8 + 8, 128:]
        rank = (lane - base) & 127
        at = jnp.zeros((8, 128), jnp.int32)
        for step in (64, 32, 16, 8, 4, 2, 1):
            seen = lanes_of(upto_here, at + (step - 1))
            at = jnp.where(seen <= rank, at + step, at)
        place[g, pl.ds(c * 8, 8), :] = at
        moved = c - ((base + rank) >> 7)
        state.append(jnp.where(rank < number, moved, 0))
        base = base + number
    count[g] = base
    arrived = [jnp.zeros((8, 128), jnp.int32) for _ in range(CHUNKS)]
    for s in range(5):
        bit = 1 << s
        new_state = []
        for c in range(CHUNKS):
            kept = jnp.where((state[c] & bit) != 0, 0, state[c])
            if c + bit < CHUNKS:
                comes = (state[c + bit] & bit) != 0
                arrived[c] = jnp.where(comes, arrived[c] | bit, arrived[c])
                kept = jnp.where(comes, state[c + bit], kept)
            new_state.append(kept)
        state = new_state
    for c in range(CHUNKS):
        arrive[g, pl.ds(c * 8, 8), :] = arrived[c]


def pack_group(f, g, landed, old, new, place, arrive, count):
    rows = pl.ds(pl.multiple_of(g * 8, 8), 8)
    value = []
    for c in range(CHUNKS):
        raw = landed[f, c // 2, rows, pl.ds((c % 2) * 128, 128)]
        value.append(lanes_of(raw, place[g, pl.ds(c * 8, 8), :]))
    moves = [arrive[g, pl.ds(c * 8, 8), :] for c in range(CHUNKS)]
    for s in range(5):
        bit = 1 << s
        for c in range(CHUNKS - bit):
            if s < 4 or c < OUT_CHUNKS:
                value[c] = jnp.where((moves[c] & bit) != 0, value[c + bit], value[c])
    lane = lax.broadcasted_iota(jnp.int32, (8, 128), 1)
    left = count[g] - lane
    squares = jnp.zeros((8, 128), jnp.float32)
    for c in range(OUT_CHUNKS):
        columns = pl.ds(c * 128, 128)
        mean = (STEPS * old[f, rows, columns] + value[c]) * jnp.float32(1.0 / (STEPS + 1.0))
        mean = jnp.where(left > c * 128, mean, jnp.float32(0.0))
        new[f, rows, columns] = mean
        squares = squares + mean * mean
    return squares


def kernel(
    fields, mean_old, land_mask, mean_new, rms,
    landed, mask, old, new, place, arrive, count, total, parts,
    send_sem, recv_sem, mask_sem, old_sem, new_sem, part_send, part_recv,
):
    io, b = lax.axis_index("io"), lax.axis_index("cmp")
    x, core = b // 2, b % 2
    keeps = (io // 2) == b

    def greet(s, carry):
        pl.semaphore_signal(barrier, inc=1, device_id=(s, io // 2), device_id_type=MESH)
        pl.semaphore_signal(barrier, inc=1, device_id=(s, b), device_id_type=MESH)
        return carry

    barrier = pltpu.get_barrier_semaphore()
    lax.fori_loop(0, LON, greet, 0)
    mask_copy = pltpu.make_async_copy(land_mask.at[0], mask, mask_sem)
    mask_copy.start()
    old_copy = pltpu.make_async_copy(mean_old.at[:, 0], old, old_sem)
    old_copy.start()
    pl.semaphore_wait(barrier, 2 * LON)

    peers = []
    for dx, dy, dc in ORDER:
        level = lax.rem(x + dx, 4) * 2 + lax.rem(core + dc, 2)
        band = x * 4 + core * 2 + dy
        peers.append((level, band, dy, (band == io) & (level == b)))

    def send_piece(i, carry):
        f, first = i // PIECES, lax.rem(i, PIECES) * PIECE_ROWS
        for level, band, half, here in peers:
            rows = pl.ds(pl.multiple_of(half * ROWS + first, 8), PIECE_ROWS)
            source = fields.at[f, level, rows, :]
            target = landed.at[f, io, pl.ds(pl.multiple_of(first, 8), PIECE_ROWS), :]

            @pl.when(jnp.logical_not(here))
            def _():
                pltpu.make_async_remote_copy(
                    src_ref=source,
                    dst_ref=target,
                    send_sem=send_sem.at[i],
                    recv_sem=recv_sem.at[i],
                    device_id=(band, level),
                    device_id_type=MESH,
                ).start()

            @pl.when(here)
            def _():
                pltpu.make_async_copy(source, target, recv_sem.at[i]).start()

        return carry

    lax.fori_loop(0, FIELDS * PIECES, send_piece, 0)

    mask_copy.wait()

    def plan(g, carry):
        plan_group(g, mask, place, arrive, count)
        return carry

    lax.fori_loop(0, GROUPS, plan, 0)
    total[...] = jnp.zeros_like(total)
    old_copy.wait()

    def pack_piece(i, carry):
        f, first = i // PIECES, lax.rem(i, PIECES) * PIECE_ROWS
        rows = pl.ds(pl.multiple_of(first, 8), PIECE_ROWS)
        piece = landed.at[f, :, rows, :]
        pltpu.make_async_copy(piece, piece, recv_sem.at[i]).wait()

        def pack(k, squares):
            g = lax.rem(i, PIECES) * PIECE_GROUPS + k
            return squares + pack_group(f, g, landed, old, new, place, arrive, count)

        total[f] += lax.fori_loop(0, PIECE_GROUPS, pack, jnp.zeros((8, 128), jnp.float32))
        pltpu.make_async_copy(new.at[f, rows, :], mean_new.at[f, 0, rows, :], new_sem.at[i]).start()
        return carry

    lax.fori_loop(0, FIELDS * PIECES, pack_piece, 0)

    ocean = count[0]
    for g in range(1, GROUPS):
        ocean = ocean + count[g]
    lines = [jnp.sum(total[f], axis=0, keepdims=True) for f in range(FIELDS)]
    lines.append(jnp.sum(ocean.astype(jnp.float32), axis=0, keepdims=True))
    lines.append(jnp.zeros((1, 128), jnp.float32))
    parts[io] = jnp.concatenate(lines, axis=0)

    def send_part(s, carry):
        to = lax.rem(io + s, LON)
        pltpu.make_async_remote_copy(
            src_ref=parts.at[io],
            dst_ref=parts.at[io],
            send_sem=part_send,
            recv_sem=part_recv,
            device_id=(to, b),
            device_id_type=MESH,
        ).start()
        return carry

    lax.fori_loop(1, LON, send_part, 0)

    def finish(i, carry):
        f, first = i // PIECES, lax.rem(i, PIECES) * PIECE_ROWS
        rows = pl.ds(pl.multiple_of(first, 8), PIECE_ROWS)
        pltpu.make_async_copy(new.at[f, rows, :], mean_new.at[f, 0, rows, :], new_sem.at[i]).wait()
        piece = landed.at[f, :, rows, :]

        @pl.when(jnp.logical_not(keeps))
        def _():
            pltpu.make_async_copy(piece, piece, send_sem.at[i]).wait()

        @pl.when(keeps)
        def _():
            most = landed.at[f, pl.ds(0, LON - 1), rows, :]
            pltpu.make_async_copy(most, most, send_sem.at[i]).wait()

        return carry

    lax.fori_loop(0, FIELDS * PIECES, finish, 0)
    others = parts.at[pl.ds(0, LON - 1)]
    pltpu.make_async_copy(others, others, part_send).wait()
    pltpu.make_async_copy(others, others, part_recv).wait()
    everything = parts[0]
    for s in range(1, LON):
        everything = everything + parts[s]
    square_sum = jnp.sum(everything[:FIELDS], axis=1, keepdims=True)
    ocean_total = everything[FIELDS : FIELDS + 1, :1]
    rms[...] = jnp.sqrt(square_sum / ocean_total + 1e-06)


def on_device(fields, mean_old, land_mask):
    pieces = FIELDS * PIECES
    return pl.pallas_call(
        kernel,
        out_shape=(
            jax.ShapeDtypeStruct(mean_old.shape, jnp.float32),
            jax.ShapeDtypeStruct((FIELDS, 1), jnp.float32),
        ),
        in_specs=[pl.BlockSpec(memory_space=pl.ANY)] * 3,
        out_specs=(pl.BlockSpec(memory_space=pl.ANY), pl.BlockSpec(memory_space=pltpu.VMEM)),
        scratch_shapes=[
            pltpu.VMEM((FIELDS, LON, ROWS, COLS), jnp.float32),
            pltpu.VMEM((ROWS, CHUNKS * 128), jnp.int32),
            pltpu.VMEM((FIELDS, ROWS, OUT_CHUNKS * 128), jnp.float32),
            pltpu.VMEM((FIELDS, ROWS, OUT_CHUNKS * 128), jnp.float32),
            pltpu.VMEM((GROUPS, CHUNKS * 8, 128), jnp.int32),
            pltpu.VMEM((GROUPS, CHUNKS * 8, 128), jnp.int32),
            pltpu.VMEM((GROUPS, 8, 128), jnp.int32),
            pltpu.VMEM((FIELDS, 8, 128), jnp.float32),
            pltpu.VMEM((LON, 8, 128), jnp.float32),
            pltpu.SemaphoreType.DMA((pieces,)),
            pltpu.SemaphoreType.DMA((pieces,)),
            pltpu.SemaphoreType.DMA,
            pltpu.SemaphoreType.DMA,
            pltpu.SemaphoreType.DMA((pieces,)),
            pltpu.SemaphoreType.DMA,
            pltpu.SemaphoreType.DMA,
        ],
        compiler_params=pltpu.CompilerParams(
            collective_id=0, has_side_effects=True, vmem_limit_bytes=56 * 1024 * 1024
        ),
    )(fields, mean_old, land_mask)


def solution(mesh):
    in_specs = (P(None, None, "cmp", "io"), P(None, "cmp", "io", None), P("cmp", "io", None))
    out_specs = (P(None, "cmp", "io", None), P(None, "cmp"))
    return jax.shard_map(
        on_device, mesh=mesh, in_specs=in_specs, out_specs=out_specs, check_vma=False
    )
```

profile of v0, /device:TPU:4, one launch (start us, length us, event | category | flops | bytes accessed | tf_op | source)
XLA Modules:
  0.0 97.6 jit_solution(10026840849086415818)
XLA Ops:
  0.6 90.7 %shard_map.50 = (f32[6,1,64,3072]{3,2,1,0:T(8,128)}, f32[6,1]{1,0:T(8,128)}) custom-call(f32[6,8,128,256]{3,2,1,0:T(8,128)} %fields.1, f32[6,1,64,3072]{3,2,1,0:T(8,128)} %mean_old.1, s32[1,64,4096]{2,1,0:T(8,128)} %land_mask.1), custom_call_target="tpu_custom_call" | custom-call | tf_op jit(solution)/shard_map/pallas_call | solution.py:225
  91.3 1.3 %copy.5 = f32[6,1]{0,1:T(1,128)} copy(f32[6,1]{1,0:T(8,128)} %get-tuple-element.3) | data formatting | bytes 48 | tf_op jit(solution)/shard_map/pallas_call | solution.py:225
  92.6 5.1 %copy.7 = f32[6,1,64,3072]{3,2,1,0:T(8,128)} copy(f32[6,1,64,3072]{3,2,1,0:T(8,128)} %get-tuple-element.6) | data formatting | bytes 9437184
where the time goes:
time: 97.8 us; the launch traced here: 97.6 us
  Pallas kernels  90.7 us (93%)
  local copies, waits for them, and re-layouts  6.32 us (6%)
    pallas_call x1, Pallas kernels, on_device(): pl.pallas_call(kernel, out_shape=(jax.ShapeDtypeStruct(mean_old.shape, jn...  90.7 us
    unnamed x1, local copies, waits for them, and re-layouts  5.05 us

commit v1 on v0

--- a/solution.py
+++ b/solution.py
@@ -18,7 +18,7 @@
 PIECE_ROWS = ROWS // PIECES
 GROUPS = ROWS // 8
 PIECE_GROUPS = PIECE_ROWS // 8
-ORDER = [(dx, dy, dc) for dy in (0, 1) for dc in (0, 1) for dx in (1, 3, 2, 0)]
+ORDER = [(dx, dy, dc) for dc in (0, 1) for dx in (1, 3, 2, 0) for dy in (0, 1)]
 
 
 def lanes_of(array, index):
@@ -84,15 +84,15 @@
         columns = pl.ds(c * 128, 128)
         mean = (STEPS * old[f, rows, columns] + value[c]) * jnp.float32(1.0 / (STEPS + 1.0))
         mean = jnp.where(left > c * 128, mean, jnp.float32(0.0))
-        new[f, rows, columns] = mean
+        new[f, 0, rows, columns] = mean
         squares = squares + mean * mean
     return squares
 
 
 def kernel(
-    fields, mean_old, land_mask, mean_new, rms,
-    landed, mask, old, new, place, arrive, count, total, parts,
-    send_sem, recv_sem, mask_sem, old_sem, new_sem, part_send, part_recv,
+    fields, mean_old, land_mask, new, rms,
+    landed, mask, old, place, arrive, count, total, parts,
+    send_sem, recv_sem, mask_sem, old_sem, part_send, part_recv,
 ):
     io, b = lax.axis_index("io"), lax.axis_index("cmp")
     x, core = b // 2, b % 2
@@ -114,8 +114,9 @@
     peers = []
     for dx, dy, dc in ORDER:
         level = lax.rem(x + dx, 4) * 2 + lax.rem(core + dc, 2)
-        band = x * 4 + core * 2 + dy
-        peers.append((level, band, dy, (band == io) & (level == b)))
+        half = lax.rem(io + io // 4 + dy, 2)
+        band = x * 4 + core * 2 + half
+        peers.append((level, band, half, (band == io) & (level == b)))
 
     def send_piece(i, carry):
         f, first = i // PIECES, lax.rem(i, PIECES) * PIECE_ROWS
@@ -164,7 +165,6 @@
             return squares + pack_group(f, g, landed, old, new, place, arrive, count)
 
         total[f] += lax.fori_loop(0, PIECE_GROUPS, pack, jnp.zeros((8, 128), jnp.float32))
-        pltpu.make_async_copy(new.at[f, rows, :], mean_new.at[f, 0, rows, :], new_sem.at[i]).start()
         return carry
 
     lax.fori_loop(0, FIELDS * PIECES, pack_piece, 0)
@@ -194,7 +194,6 @@
     def finish(i, carry):
         f, first = i // PIECES, lax.rem(i, PIECES) * PIECE_ROWS
         rows = pl.ds(pl.multiple_of(first, 8), PIECE_ROWS)
-        pltpu.make_async_copy(new.at[f, rows, :], mean_new.at[f, 0, rows, :], new_sem.at[i]).wait()
         piece = landed.at[f, :, rows, :]
 
         @pl.when(jnp.logical_not(keeps))
@@ -215,25 +214,44 @@
     everything = parts[0]
     for s in range(1, LON):
         everything = everything + parts[s]
-    square_sum = jnp.sum(everything[:FIELDS], axis=1, keepdims=True)
-    ocean_total = everything[FIELDS : FIELDS + 1, :1]
+    lane = lax.broadcasted_iota(jnp.int32, (1, 128), 1)
+    square_sum = jnp.zeros((1, 128), jnp.float32)
+    for f in range(FIELDS):
+        field_sum = jnp.sum(everything[f : f + 1], axis=1, keepdims=True)
+        square_sum = jnp.where(lane == f, field_sum, square_sum)
+    ocean_total = everything[FIELDS : FIELDS + 1]
     rms[...] = jnp.sqrt(square_sum / ocean_total + 1e-06)
+
+
+def write(new, rms, mean_new, level_rms, sem):
+    def piece(i):
+        f, first = i // PIECES, lax.rem(i, PIECES) * PIECE_ROWS
+        rows = pl.ds(pl.multiple_of(first, 8), PIECE_ROWS)
+        return pltpu.make_async_copy(new.at[f, 0, rows, :], mean_new.at[f, 0, rows, :], sem.at[i])
+
+    for i in range(FIELDS * PIECES):
+        piece(i).start()
+    level_rms[...] = rms[:, :FIELDS]
+    for i in range(FIELDS * PIECES):
+        piece(i).wait()
 
 
 def on_device(fields, mean_old, land_mask):
     pieces = FIELDS * PIECES
-    return pl.pallas_call(
+    fields, mean_old, land_mask = (
+        pltpu.with_memory_space_constraint(a, pltpu.HBM) for a in (fields, mean_old, land_mask)
+    )
+    new, rms = pl.pallas_call(
         kernel,
         out_shape=(
-            jax.ShapeDtypeStruct(mean_old.shape, jnp.float32),
-            jax.ShapeDtypeStruct((FIELDS, 1), jnp.float32),
+            pltpu.VMEM(mean_old.shape, jnp.float32),
+            pltpu.VMEM((1, 128), jnp.float32),
         ),
-        in_specs=[pl.BlockSpec(memory_space=pl.ANY)] * 3,
-        out_specs=(pl.BlockSpec(memory_space=pl.ANY), pl.BlockSpec(memory_space=pltpu.VMEM)),
+        in_specs=[pl.BlockSpec(memory_space=pltpu.HBM)] * 3,
+        out_specs=[pl.BlockSpec(memory_space=pltpu.VMEM)] * 2,
         scratch_shapes=[
             pltpu.VMEM((FIELDS, LON, ROWS, COLS), jnp.float32),
             pltpu.VMEM((ROWS, CHUNKS * 128), jnp.int32),
-            pltpu.VMEM((FIELDS, ROWS, OUT_CHUNKS * 128), jnp.float32),
             pltpu.VMEM((FIELDS, ROWS, OUT_CHUNKS * 128), jnp.float32),
             pltpu.VMEM((GROUPS, CHUNKS * 8, 128), jnp.int32),
             pltpu.VMEM((GROUPS, CHUNKS * 8, 128), jnp.int32),
@@ -244,14 +262,25 @@
             pltpu.SemaphoreType.DMA((pieces,)),
             pltpu.SemaphoreType.DMA,
             pltpu.SemaphoreType.DMA,
-            pltpu.SemaphoreType.DMA((pieces,)),
             pltpu.SemaphoreType.DMA,
             pltpu.SemaphoreType.DMA,
         ],
         compiler_params=pltpu.CompilerParams(
-            collective_id=0, has_side_effects=True, vmem_limit_bytes=56 * 1024 * 1024
+            collective_id=0, has_side_effects=True, vmem_limit_bytes=20 * 1024 * 1024
         ),
     )(fields, mean_old, land_mask)
+    mean_new, level_rms = pl.pallas_call(
+        write,
+        out_shape=(
+            jax.ShapeDtypeStruct(mean_old.shape, jnp.float32),
+            jax.ShapeDtypeStruct((1, FIELDS), jnp.float32),
+        ),
+        in_specs=[pl.BlockSpec(memory_space=pltpu.VMEM)] * 2,
+        out_specs=(pl.BlockSpec(memory_space=pltpu.HBM), pl.BlockSpec(memory_space=pltpu.VMEM)),
+        scratch_shapes=[pltpu.SemaphoreType.DMA((pieces,))],
+        compiler_params=pltpu.CompilerParams(vmem_limit_bytes=8 * 1024 * 1024),
+    )(new, rms)
+    return mean_new, level_rms.reshape(FIELDS, 1)
 
 
 def solution(mesh):

time: 97.8 us -> 91.2 us (0.933)
  the two profiles are of different devices: /device:TPU:4 before, /device:TPU:0 now
where the time goes in v1:
time: 91.2 us; the launch traced here: 91.1 us
  Pallas kernels  90.5 us (99%)
    pallas_call x1, Pallas kernels, on_device(): pl.pallas_call(kernel, out_shape=(pltpu.VMEM(mean_old.shape, jnp.float32)...  87.7 us
    pallas_call x1, Pallas kernels, on_device(): pl.pallas_call(write, out_shape=(jax.ShapeDtypeStruct(mean_old.shape, jnp...  2.78 us

profile of v1, /device:TPU:0, one launch (start us, length us, event | category | flops | bytes accessed | tf_op | source)
XLA Modules:
  0.0 91.1 jit_solution(15579201921071538660)
XLA Ops:
  0.6 87.7 %shard_map.50 = (f32[6,1,64,3072]{3,2,1,0:T(8,128)S(1)}, f32[1,128]{1,0:T(1,128)S(1)}) custom-call(f32[6,8,128,256]{3,2,1,0:T(8,128)} %fields.1, f32[6,1,64,3072]{3,2,1,0:T(8,128)} %mean_old.1, s32[1,64,4096]{2,1,0:T(8,128)} %land_mask.1), custom_call_target="tpu_custom_call" | custom-call | tf_op jit(solution)/shard_map/pallas_call | solution.py:244
  88.3 2.8 %shard_map.51 = (f32[6,1,64,3072]{3,2,1,0:T(8,128)}, f32[1,6]{1,0:T(1,128)}) custom-call(f32[6,1,64,3072]{3,2,1,0:T(8,128)S(1)} %get-tuple-element.6.new, f32[1,128]{1,0:T(1,128)S(1)} %get-tuple-element.7.rms), custom_call_target="tpu_custom_call" | custom-call | tf_op jit(solution)/shard_map/pallas_call | solution.py:272

commit v2 on v1

--- a/solution.py
+++ b/solution.py
@@ -14,10 +14,12 @@
 COLS = 256
 CHUNKS = 32
 OUT_CHUNKS = 24
-PIECES = 2
-PIECE_ROWS = ROWS // PIECES
 GROUPS = ROWS // 8
-PIECE_GROUPS = PIECE_ROWS // 8
+LAST = FIELDS - 1
+MAIN_ROWS, LAST_ROWS = 16, 8
+PER_FIELD = ROWS // MAIN_ROWS
+LAST_PIECES = MAIN_ROWS // LAST_ROWS
+ARRIVALS = LAST + PER_FIELD - 1 + LAST_PIECES
 ORDER = [(dx, dy, dc) for dc in (0, 1) for dx in (1, 3, 2, 0) for dy in (0, 1)]
 
 
@@ -90,26 +92,44 @@
 
 
 def kernel(
-    fields, mean_old, land_mask, new, rms,
-    landed, mask, old, place, arrive, count, total, parts,
-    send_sem, recv_sem, mask_sem, old_sem, part_send, part_recv,
+    fields, mean_old, land_mask, new, sums,
+    staged, landed, mask, old, place, arrive, count, total, parts,
+    stage_sem, send_sem, recv_sem, mask_sem, old_sem, part_send, part_recv,
 ):
     io, b = lax.axis_index("io"), lax.axis_index("cmp")
     x, core = b // 2, b % 2
     keeps = (io // 2) == b
 
-    def greet(s, carry):
+    barrier = pltpu.get_barrier_semaphore()
+    for s in range(LON):
         pl.semaphore_signal(barrier, inc=1, device_id=(s, io // 2), device_id_type=MESH)
+    for s in range(LON):
         pl.semaphore_signal(barrier, inc=1, device_id=(s, b), device_id_type=MESH)
-        return carry
-
-    barrier = pltpu.get_barrier_semaphore()
-    lax.fori_loop(0, LON, greet, 0)
+    def stage(f, first, size, sem):
+        return [
+            pltpu.make_async_copy(
+                fields.at[f, :, pl.ds(half * ROWS + first, size), :],
+                staged.at[f, :, pl.ds(half * ROWS + first, size), :],
+                stage_sem.at[sem],
+            )
+            for half in range(2)
+        ]
+
+    def staged_wait(f, size, sem):
+        both = staged.at[f, :, pl.ds(0, 2 * size), :]
+        pltpu.make_async_copy(both, both, stage_sem.at[sem]).wait()
+
+    for copy in stage(0, 0, MAIN_ROWS, 0):
+        copy.start()
     mask_copy = pltpu.make_async_copy(land_mask.at[0], mask, mask_sem)
     mask_copy.start()
+    for copy in stage(0, MAIN_ROWS, ROWS - MAIN_ROWS, 1):
+        copy.start()
+    for f in range(1, FIELDS):
+        for copy in stage(f, 0, ROWS, 2):
+            copy.start()
     old_copy = pltpu.make_async_copy(mean_old.at[:, 0], old, old_sem)
     old_copy.start()
-    pl.semaphore_wait(barrier, 2 * LON)
 
     peers = []
     for dx, dy, dc in ORDER:
@@ -118,31 +138,47 @@
         band = x * 4 + core * 2 + half
         peers.append((level, band, half, (band == io) & (level == b)))
 
-    def send_piece(i, carry):
-        f, first = i // PIECES, lax.rem(i, PIECES) * PIECE_ROWS
+    def send_piece(arrival, f, first, size):
         for level, band, half, here in peers:
-            rows = pl.ds(pl.multiple_of(half * ROWS + first, 8), PIECE_ROWS)
-            source = fields.at[f, level, rows, :]
-            target = landed.at[f, io, pl.ds(pl.multiple_of(first, 8), PIECE_ROWS), :]
+            rows = pl.ds(pl.multiple_of(half * ROWS + first, 8), size)
+            target = landed.at[f, io, pl.ds(pl.multiple_of(first, 8), size), :]
 
             @pl.when(jnp.logical_not(here))
             def _():
                 pltpu.make_async_remote_copy(
-                    src_ref=source,
+                    src_ref=staged.at[f, level, rows, :],
                     dst_ref=target,
-                    send_sem=send_sem.at[i],
-                    recv_sem=recv_sem.at[i],
+                    send_sem=send_sem,
+                    recv_sem=recv_sem.at[arrival],
                     device_id=(band, level),
                     device_id_type=MESH,
                 ).start()
 
             @pl.when(here)
             def _():
-                pltpu.make_async_copy(source, target, recv_sem.at[i]).start()
-
-        return carry
-
-    lax.fori_loop(0, FIELDS * PIECES, send_piece, 0)
+                pltpu.make_async_copy(fields.at[f, level, rows, :], target, recv_sem.at[arrival]).start()
+
+    def send_early(i, carry):
+        f = i // PER_FIELD
+        send_piece(f, f, lax.rem(i, PER_FIELD) * MAIN_ROWS, MAIN_ROWS)
+        return carry
+
+    def send_late(i, carry):
+        send_piece(LAST + i, LAST, i * MAIN_ROWS, MAIN_ROWS)
+        return carry
+
+    staged_wait(0, MAIN_ROWS, 0)
+    pl.semaphore_wait(barrier, 2 * LON)
+    send_early(0, 0)
+    staged_wait(0, ROWS - MAIN_ROWS, 1)
+    lax.fori_loop(1, PER_FIELD, send_early, 0)
+    others = staged.at[pl.ds(1, FIELDS - 1)]
+    pltpu.make_async_copy(others, others, stage_sem.at[2]).wait()
+    lax.fori_loop(PER_FIELD, LAST * PER_FIELD, send_early, 0)
+    lax.fori_loop(0, PER_FIELD - 1, send_late, 0)
+    for i in range(LAST_PIECES):
+        first = ROWS - MAIN_ROWS + i * LAST_ROWS
+        send_piece(LAST + PER_FIELD - 1 + i, LAST, first, LAST_ROWS)
 
     mask_copy.wait()
 
@@ -154,20 +190,30 @@
     total[...] = jnp.zeros_like(total)
     old_copy.wait()
 
-    def pack_piece(i, carry):
-        f, first = i // PIECES, lax.rem(i, PIECES) * PIECE_ROWS
-        rows = pl.ds(pl.multiple_of(first, 8), PIECE_ROWS)
-        piece = landed.at[f, :, rows, :]
-        pltpu.make_async_copy(piece, piece, recv_sem.at[i]).wait()
+    def pack_piece(arrival, f, first, size):
+        piece = landed.at[f, :, pl.ds(pl.multiple_of(first, 8), size), :]
+        pltpu.make_async_copy(piece, piece, recv_sem.at[arrival]).wait()
 
         def pack(k, squares):
-            g = lax.rem(i, PIECES) * PIECE_GROUPS + k
-            return squares + pack_group(f, g, landed, old, new, place, arrive, count)
-
-        total[f] += lax.fori_loop(0, PIECE_GROUPS, pack, jnp.zeros((8, 128), jnp.float32))
-        return carry
-
-    lax.fori_loop(0, FIELDS * PIECES, pack_piece, 0)
+            return squares + pack_group(f, first // 8 + k, landed, old, new, place, arrive, count)
+
+        total[f] += lax.fori_loop(0, size // 8, pack, jnp.zeros((8, 128), jnp.float32))
+
+    def pack_early(f, carry):
+        pack_piece(f, f, 0, ROWS)
+        return carry
+
+    def pack_late(i, carry):
+        pack_piece(LAST + i, LAST, i * MAIN_ROWS, MAIN_ROWS)
+        return carry
+
+    def pack_last(i, carry):
+        pack_piece(LAST + PER_FIELD - 1 + i, LAST, ROWS - MAIN_ROWS + i * LAST_ROWS, LAST_ROWS)
+        return carry
+
+    lax.fori_loop(0, LAST, pack_early, 0)
+    lax.fori_loop(0, PER_FIELD - 1, pack_late, 0)
+    lax.fori_loop(0, LAST_PIECES, pack_last, 0)
 
     ocean = count[0]
     for g in range(1, GROUPS):
@@ -191,65 +237,51 @@
 
     lax.fori_loop(1, LON, send_part, 0)
 
-    def finish(i, carry):
-        f, first = i // PIECES, lax.rem(i, PIECES) * PIECE_ROWS
-        rows = pl.ds(pl.multiple_of(first, 8), PIECE_ROWS)
-        piece = landed.at[f, :, rows, :]
-
-        @pl.when(jnp.logical_not(keeps))
-        def _():
-            pltpu.make_async_copy(piece, piece, send_sem.at[i]).wait()
-
-        @pl.when(keeps)
-        def _():
-            most = landed.at[f, pl.ds(0, LON - 1), rows, :]
-            pltpu.make_async_copy(most, most, send_sem.at[i]).wait()
-
-        return carry
-
-    lax.fori_loop(0, FIELDS * PIECES, finish, 0)
+    @pl.when(jnp.logical_not(keeps))
+    def _():
+        pltpu.make_async_copy(landed, landed, send_sem).wait()
+
+    @pl.when(keeps)
+    def _():
+        most = landed.at[:, pl.ds(0, LON - 1)]
+        pltpu.make_async_copy(most, most, send_sem).wait()
+
     others = parts.at[pl.ds(0, LON - 1)]
     pltpu.make_async_copy(others, others, part_send).wait()
     pltpu.make_async_copy(others, others, part_recv).wait()
     everything = parts[0]
     for s in range(1, LON):
         everything = everything + parts[s]
+    sums[...] = everything
+
+
+def write(new, sums, mean_new, level_rms, sem):
+    for f in range(FIELDS):
+        pltpu.make_async_copy(new.at[f], mean_new.at[f], sem).start()
     lane = lax.broadcasted_iota(jnp.int32, (1, 128), 1)
     square_sum = jnp.zeros((1, 128), jnp.float32)
     for f in range(FIELDS):
-        field_sum = jnp.sum(everything[f : f + 1], axis=1, keepdims=True)
+        field_sum = jnp.sum(sums[f : f + 1], axis=1, keepdims=True)
         square_sum = jnp.where(lane == f, field_sum, square_sum)
-    ocean_total = everything[FIELDS : FIELDS + 1]
-    rms[...] = jnp.sqrt(square_sum / ocean_total + 1e-06)
-
-
-def write(new, rms, mean_new, level_rms, sem):
-    def piece(i):
-        f, first = i // PIECES, lax.rem(i, PIECES) * PIECE_ROWS
-        rows = pl.ds(pl.multiple_of(first, 8), PIECE_ROWS)
-        return pltpu.make_async_copy(new.at[f, 0, rows, :], mean_new.at[f, 0, rows, :], sem.at[i])
-
-    for i in range(FIELDS * PIECES):
-        piece(i).start()
-    level_rms[...] = rms[:, :FIELDS]
-    for i in range(FIELDS * PIECES):
-        piece(i).wait()
+    ocean_total = sums[FIELDS : FIELDS + 1]
+    level_rms[...] = jnp.sqrt(square_sum / ocean_total + 1e-06)[:, :FIELDS]
+    pltpu.make_async_copy(new, mean_new, sem).wait()
 
 
 def on_device(fields, mean_old, land_mask):
-    pieces = FIELDS * PIECES
     fields, mean_old, land_mask = (
         pltpu.with_memory_space_constraint(a, pltpu.HBM) for a in (fields, mean_old, land_mask)
     )
-    new, rms = pl.pallas_call(
+    new, sums = pl.pallas_call(
         kernel,
         out_shape=(
             pltpu.VMEM(mean_old.shape, jnp.float32),
-            pltpu.VMEM((1, 128), jnp.float32),
+            pltpu.VMEM((8, 128), jnp.float32),
         ),
         in_specs=[pl.BlockSpec(memory_space=pltpu.HBM)] * 3,
         out_specs=[pl.BlockSpec(memory_space=pltpu.VMEM)] * 2,
         scratch_shapes=[
+            pltpu.VMEM(fields.shape, jnp.float32),
             pltpu.VMEM((FIELDS, LON, ROWS, COLS), jnp.float32),
             pltpu.VMEM((ROWS, CHUNKS * 128), jnp.int32),
             pltpu.VMEM((FIELDS, ROWS, OUT_CHUNKS * 128), jnp.float32),
@@ -258,15 +290,16 @@
             pltpu.VMEM((GROUPS, 8, 128), jnp.int32),
             pltpu.VMEM((FIELDS, 8, 128), jnp.float32),
             pltpu.VMEM((LON, 8, 128), jnp.float32),
-            pltpu.SemaphoreType.DMA((pieces,)),
-            pltpu.SemaphoreType.DMA((pieces,)),
+            pltpu.SemaphoreType.DMA((3,)),
+            pltpu.SemaphoreType.DMA,
+            pltpu.SemaphoreType.DMA((ARRIVALS,)),
             pltpu.SemaphoreType.DMA,
             pltpu.SemaphoreType.DMA,
             pltpu.SemaphoreType.DMA,
             pltpu.SemaphoreType.DMA,
         ],
         compiler_params=pltpu.CompilerParams(
-            collective_id=0, has_side_effects=True, vmem_limit_bytes=20 * 1024 * 1024
+            collective_id=0, has_side_effects=True, vmem_limit_bytes=28 * 1024 * 1024
         ),
     )(fields, mean_old, land_mask)
     mean_new, level_rms = pl.pallas_call(
@@ -277,9 +310,9 @@
         ),
         in_specs=[pl.BlockSpec(memory_space=pltpu.VMEM)] * 2,
         out_specs=(pl.BlockSpec(memory_space=pltpu.HBM), pl.BlockSpec(memory_space=pltpu.VMEM)),
-        scratch_shapes=[pltpu.SemaphoreType.DMA((pieces,))],
+        scratch_shapes=[pltpu.SemaphoreType.DMA],
         compiler_params=pltpu.CompilerParams(vmem_limit_bytes=8 * 1024 * 1024),
-    )(new, rms)
+    )(new, sums)
     return mean_new, level_rms.reshape(FIELDS, 1)
 
 

time: 91.2 us -> 89.3 us (0.979)
  Pallas kernels: 90.5 us -> 88.5 us
    pallas_call x1, Pallas kernels: 87.7 us -> 85.8 us  [on_device(): pl.pallas_call(kernel, out_shape=(pltpu.VMEM(mean_old.shape, jnp.float32)...]
where the time goes in v2:
time: 89.3 us; the launch traced here: 89.2 us
  Pallas kernels  88.5 us (99%)
    pallas_call x1, Pallas kernels, on_device(): pl.pallas_call(kernel, out_shape=(pltpu.VMEM(mean_old.shape, jnp.float32)...  85.8 us
    pallas_call x1, Pallas kernels, on_device(): pl.pallas_call(write, out_shape=(jax.ShapeDtypeStruct(mean_old.shape, jnp...  2.69 us

profile of v2, /device:TPU:0, one launch (start us, length us, event | category | flops | bytes accessed | tf_op | source)
XLA Modules:
  0.0 89.2 jit_solution(1143121946281639377)
XLA Ops:
  0.6 85.8 %shard_map.50 = (f32[6,1,64,3072]{3,2,1,0:T(8,128)S(1)}, f32[8,128]{1,0:T(8,128)S(1)}) custom-call(f32[6,8,128,256]{3,2,1,0:T(8,128)} %fields.1, f32[6,1,64,3072]{3,2,1,0:T(8,128)} %mean_old.1, s32[1,64,4096]{2,1,0:T(8,128)} %land_mask.1), custom_call_target="tpu_custom_call" | custom-call | tf_op jit(solution)/shard_map/pallas_call | solution.py:275
  86.5 2.7 %shard_map.51 = (f32[6,1,64,3072]{3,2,1,0:T(8,128)}, f32[1,6]{1,0:T(1,128)}) custom-call(f32[6,1,64,3072]{3,2,1,0:T(8,128)S(1)} %get-tuple-element.6.new, f32[8,128]{1,0:T(8,128)S(1)} %get-tuple-element.7.sums), custom_call_target="tpu_custom_call" | custom-call | tf_op jit(solution)/shard_map/pallas_call | solution.py:305

commit v3 on v2

--- a/solution.py
+++ b/solution.py
@@ -20,7 +20,14 @@
 PER_FIELD = ROWS // MAIN_ROWS
 LAST_PIECES = MAIN_ROWS // LAST_ROWS
 ARRIVALS = LAST + PER_FIELD - 1 + LAST_PIECES
-ORDER = [(dx, dy, dc) for dc in (0, 1) for dx in (1, 3, 2, 0) for dy in (0, 1)]
+ORDER = [(dx, dy, dc) for dc in (0, 1) for dx in (2, 1, 3, 0) for dy in (0, 1)]
+
+
+RING_HOPS = (0, 1, 2, 1)
+FAR_FIRST = sorted(
+    ((dz, dy) for dz in range(4) for dy in range(4) if (dz, dy) != (0, 0)),
+    key=lambda d: -RING_HOPS[d[0]] - RING_HOPS[d[1]],
+)
 
 
 def lanes_of(array, index):
@@ -134,7 +141,7 @@
     peers = []
     for dx, dy, dc in ORDER:
         level = lax.rem(x + dx, 4) * 2 + lax.rem(core + dc, 2)
-        half = lax.rem(io + io // 4 + dy, 2)
+        half = lax.rem((lax.rem(io, 4) + 1) // 2 + 1 + core + dy, 2)
         band = x * 4 + core * 2 + half
         peers.append((level, band, half, (band == io) & (level == b)))
 
@@ -223,8 +230,8 @@
     lines.append(jnp.zeros((1, 128), jnp.float32))
     parts[io] = jnp.concatenate(lines, axis=0)
 
-    def send_part(s, carry):
-        to = lax.rem(io + s, LON)
+    for dz, dy in FAR_FIRST:
+        to = lax.rem(io // 4 + dz, 4) * 4 + lax.rem(lax.rem(io, 4) + dy, 4)
         pltpu.make_async_remote_copy(
             src_ref=parts.at[io],
             dst_ref=parts.at[io],
@@ -233,9 +240,6 @@
             device_id=(to, b),
             device_id_type=MESH,
         ).start()
-        return carry
-
-    lax.fori_loop(1, LON, send_part, 0)
 
     @pl.when(jnp.logical_not(keeps))
     def _():
@@ -255,17 +259,20 @@
     sums[...] = everything
 
 
-def write(new, sums, mean_new, level_rms, sem):
+def write(new, sums, mean_new, level_rms, row, mean_sem, row_sem):
     for f in range(FIELDS):
-        pltpu.make_async_copy(new.at[f], mean_new.at[f], sem).start()
+        pltpu.make_async_copy(new.at[f], mean_new.at[f], mean_sem).start()
     lane = lax.broadcasted_iota(jnp.int32, (1, 128), 1)
     square_sum = jnp.zeros((1, 128), jnp.float32)
     for f in range(FIELDS):
         field_sum = jnp.sum(sums[f : f + 1], axis=1, keepdims=True)
         square_sum = jnp.where(lane == f, field_sum, square_sum)
     ocean_total = sums[FIELDS : FIELDS + 1]
-    level_rms[...] = jnp.sqrt(square_sum / ocean_total + 1e-06)[:, :FIELDS]
-    pltpu.make_async_copy(new, mean_new, sem).wait()
+    row[...] = jnp.sqrt(square_sum / ocean_total + 1e-06)[:, :FIELDS]
+    row_copy = pltpu.make_async_copy(row, level_rms, row_sem)
+    row_copy.start()
+    pltpu.make_async_copy(new, mean_new, mean_sem).wait()
+    row_copy.wait()
 
 
 def on_device(fields, mean_old, land_mask):
@@ -309,8 +316,12 @@
             jax.ShapeDtypeStruct((1, FIELDS), jnp.float32),
         ),
         in_specs=[pl.BlockSpec(memory_space=pltpu.VMEM)] * 2,
-        out_specs=(pl.BlockSpec(memory_space=pltpu.HBM), pl.BlockSpec(memory_space=pltpu.VMEM)),
-        scratch_shapes=[pltpu.SemaphoreType.DMA],
+        out_specs=[pl.BlockSpec(memory_space=pltpu.HBM)] * 2,
+        scratch_shapes=[
+            pltpu.VMEM((1, FIELDS), jnp.float32),
+            pltpu.SemaphoreType.DMA,
+            pltpu.SemaphoreType.DMA,
+        ],
         compiler_params=pltpu.CompilerParams(vmem_limit_bytes=8 * 1024 * 1024),
     )(new, sums)
     return mean_new, level_rms.reshape(FIELDS, 1)

time: 89.3 us -> 88.7 us (level)
  no operation moved by 1% of the time
where the time goes in v3:
time: 88.7 us; the launch traced here: 88.6 us
  Pallas kernels  87.9 us (99%)
    pallas_call x1, Pallas kernels, on_device(): pl.pallas_call(kernel, out_shape=(pltpu.VMEM(mean_old.shape, jnp.float32)...  85.7 us
    pallas_call x1, Pallas kernels, on_device(): pl.pallas_call(write, out_shape=(jax.ShapeDtypeStruct(mean_old.shape, jnp...  2.19 us

profile of v3, /device:TPU:0, one launch (start us, length us, event | category | flops | bytes accessed | tf_op | source)
XLA Modules:
  0.0 88.6 jit_solution(1352058894597401522)
XLA Ops:
  0.6 85.7 %shard_map.50 = (f32[6,1,64,3072]{3,2,1,0:T(8,128)S(1)}, f32[8,128]{1,0:T(8,128)S(1)}) custom-call(f32[6,8,128,256]{3,2,1,0:T(8,128)} %fields.1, f32[6,1,64,3072]{3,2,1,0:T(8,128)} %mean_old.1, s32[1,64,4096]{2,1,0:T(8,128)} %land_mask.1), custom_call_target="tpu_custom_call" | custom-call | tf_op jit(solution)/shard_map/pallas_call | solution.py:282
  86.4 2.2 %shard_map.51 = (f32[6,1,64,3072]{3,2,1,0:T(8,128)}, f32[1,6]{1,0:T(1,128)}) custom-call(f32[6,1,64,3072]{3,2,1,0:T(8,128)S(1)} %get-tuple-element.6.new, f32[8,128]{1,0:T(8,128)S(1)} %get-tuple-element.7.sums), custom_call_target="tpu_custom_call" | custom-call | tf_op jit(solution)/shard_map/pallas_call | solution.py:312

commit v4 on v3

--- a/solution.py
+++ b/solution.py
@@ -101,7 +101,7 @@
 def kernel(
     fields, mean_old, land_mask, new, sums,
     staged, landed, mask, old, place, arrive, count, total, parts,
-    stage_sem, send_sem, recv_sem, mask_sem, old_sem, part_send, part_recv,
+    stage_sem, send_sem, recv_sem, mask_sem, old_sem, part_send, part_recv, group_sem,
 ):
     io, b = lax.axis_index("io"), lax.axis_index("cmp")
     x, core = b // 2, b % 2
@@ -110,8 +110,6 @@
     barrier = pltpu.get_barrier_semaphore()
     for s in range(LON):
         pl.semaphore_signal(barrier, inc=1, device_id=(s, io // 2), device_id_type=MESH)
-    for s in range(LON):
-        pl.semaphore_signal(barrier, inc=1, device_id=(s, b), device_id_type=MESH)
     def stage(f, first, size, sem):
         return [
             pltpu.make_async_copy(
@@ -175,7 +173,7 @@
         return carry
 
     staged_wait(0, MAIN_ROWS, 0)
-    pl.semaphore_wait(barrier, 2 * LON)
+    pl.semaphore_wait(barrier, LON)
     send_early(0, 0)
     staged_wait(0, ROWS - MAIN_ROWS, 1)
     lax.fori_loop(1, PER_FIELD, send_early, 0)
@@ -218,7 +216,14 @@
         pack_piece(LAST + PER_FIELD - 1 + i, LAST, ROWS - MAIN_ROWS + i * LAST_ROWS, LAST_ROWS)
         return carry
 
-    lax.fori_loop(0, LAST, pack_early, 0)
+    pack_early(0, 0)
+
+    @pl.when(io == 2 * b)
+    def _():
+        for s in range(LON):
+            pl.semaphore_signal(group_sem, inc=1, device_id=(s, b), device_id_type=MESH)
+
+    lax.fori_loop(1, LAST, pack_early, 0)
     lax.fori_loop(0, PER_FIELD - 1, pack_late, 0)
     lax.fori_loop(0, LAST_PIECES, pack_last, 0)
 
@@ -230,6 +235,7 @@
     lines.append(jnp.zeros((1, 128), jnp.float32))
     parts[io] = jnp.concatenate(lines, axis=0)
 
+    pl.semaphore_wait(group_sem, 1)
     for dz, dy in FAR_FIRST:
         to = lax.rem(io // 4 + dz, 4) * 4 + lax.rem(lax.rem(io, 4) + dy, 4)
         pltpu.make_async_remote_copy(
@@ -304,6 +310,7 @@
             pltpu.SemaphoreType.DMA,
             pltpu.SemaphoreType.DMA,
             pltpu.SemaphoreType.DMA,
+            pltpu.SemaphoreType.REGULAR,
         ],
         compiler_params=pltpu.CompilerParams(
             collective_id=0, has_side_effects=True, vmem_limit_bytes=28 * 1024 * 1024

time: 88.7 us -> 88.2 us (level)
  no operation moved by 1% of the time
where the time goes in v4:
time: 88.2 us; the launch traced here: 88.1 us
  Pallas kernels  87.4 us (99%)
    pallas_call x1, Pallas kernels, on_device(): pl.pallas_call(kernel, out_shape=(pltpu.VMEM(mean_old.shape, jnp.float32)...  85.2 us
    pallas_call x1, Pallas kernels, on_device(): pl.pallas_call(write, out_shape=(jax.ShapeDtypeStruct(mean_old.shape, jnp...  2.19 us

profile of v4, /device:TPU:0, one launch (start us, length us, event | category | flops | bytes accessed | tf_op | source)
XLA Modules:
  0.0 88.1 jit_solution(12036248179735057784)
XLA Ops:
  0.6 85.2 %shard_map.50 = (f32[6,1,64,3072]{3,2,1,0:T(8,128)S(1)}, f32[8,128]{1,0:T(8,128)S(1)}) custom-call(f32[6,8,128,256]{3,2,1,0:T(8,128)} %fields.1, f32[6,1,64,3072]{3,2,1,0:T(8,128)} %mean_old.1, s32[1,64,4096]{2,1,0:T(8,128)} %land_mask.1), custom_call_target="tpu_custom_call" | custom-call | tf_op jit(solution)/shard_map/pallas_call | solution.py:288
  85.9 2.2 %shard_map.51 = (f32[6,1,64,3072]{3,2,1,0:T(8,128)}, f32[1,6]{1,0:T(1,128)}) custom-call(f32[6,1,64,3072]{3,2,1,0:T(8,128)S(1)} %get-tuple-element.6.new, f32[8,128]{1,0:T(8,128)S(1)} %get-tuple-element.7.sums), custom_call_target="tpu_custom_call" | custom-call | tf_op jit(solution)/shard_map/pallas_call | solution.py:319

commit v5 on v4

--- a/solution.py
+++ b/solution.py
@@ -16,10 +16,10 @@
 OUT_CHUNKS = 24
 GROUPS = ROWS // 8
 LAST = FIELDS - 1
-MAIN_ROWS, LAST_ROWS = 16, 8
-PER_FIELD = ROWS // MAIN_ROWS
-LAST_PIECES = MAIN_ROWS // LAST_ROWS
-ARRIVALS = LAST + PER_FIELD - 1 + LAST_PIECES
+PIECE_ROWS = 8
+PER_FIELD = ROWS // PIECE_ROWS
+LATE = ((0, 32), (32, 16), (48, 8), (56, 8))
+ARRIVALS = LAST + len(LATE)
 ORDER = [(dx, dy, dc) for dc in (0, 1) for dx in (2, 1, 3, 0) for dy in (0, 1)]
 
 
@@ -28,6 +28,14 @@
     ((dz, dy) for dz in range(4) for dy in range(4) if (dz, dy) != (0, 0)),
     key=lambda d: -RING_HOPS[d[0]] - RING_HOPS[d[1]],
 )
+
+
+def band_at(io, dz, dy):
+    return lax.rem(io // 4 + dz, 4) * 4 + lax.rem(lax.rem(io, 4) + dy, 4)
+
+
+def at_eight(row):
+    return row if isinstance(row, int) else pl.multiple_of(row, 8)
 
 
 def lanes_of(array, index):
@@ -108,8 +116,10 @@
     keeps = (io // 2) == b
 
     barrier = pltpu.get_barrier_semaphore()
-    for s in range(LON):
-        pl.semaphore_signal(barrier, inc=1, device_id=(s, io // 2), device_id_type=MESH)
+    for dz, dy in FAR_FIRST + [(0, 0)]:
+        pl.semaphore_signal(
+            barrier, inc=1, device_id=(band_at(io, dz, dy), io // 2), device_id_type=MESH
+        )
     def stage(f, first, size, sem):
         return [
             pltpu.make_async_copy(
@@ -124,11 +134,11 @@
         both = staged.at[f, :, pl.ds(0, 2 * size), :]
         pltpu.make_async_copy(both, both, stage_sem.at[sem]).wait()
 
-    for copy in stage(0, 0, MAIN_ROWS, 0):
+    for copy in stage(0, 0, PIECE_ROWS, 0):
         copy.start()
     mask_copy = pltpu.make_async_copy(land_mask.at[0], mask, mask_sem)
     mask_copy.start()
-    for copy in stage(0, MAIN_ROWS, ROWS - MAIN_ROWS, 1):
+    for copy in stage(0, PIECE_ROWS, ROWS - PIECE_ROWS, 1):
         copy.start()
     for f in range(1, FIELDS):
         for copy in stage(f, 0, ROWS, 2):
@@ -146,7 +156,7 @@
     def send_piece(arrival, f, first, size):
         for level, band, half, here in peers:
             rows = pl.ds(pl.multiple_of(half * ROWS + first, 8), size)
-            target = landed.at[f, io, pl.ds(pl.multiple_of(first, 8), size), :]
+            target = landed.at[f, io, pl.ds(at_eight(first), size), :]
 
             @pl.when(jnp.logical_not(here))
             def _():
@@ -165,25 +175,24 @@
 
     def send_early(i, carry):
         f = i // PER_FIELD
-        send_piece(f, f, lax.rem(i, PER_FIELD) * MAIN_ROWS, MAIN_ROWS)
+        send_piece(f, f, lax.rem(i, PER_FIELD) * PIECE_ROWS, PIECE_ROWS)
         return carry
 
-    def send_late(i, carry):
-        send_piece(LAST + i, LAST, i * MAIN_ROWS, MAIN_ROWS)
-        return carry
-
-    staged_wait(0, MAIN_ROWS, 0)
+    staged_wait(0, PIECE_ROWS, 0)
     pl.semaphore_wait(barrier, LON)
     send_early(0, 0)
-    staged_wait(0, ROWS - MAIN_ROWS, 1)
+    staged_wait(0, ROWS - PIECE_ROWS, 1)
     lax.fori_loop(1, PER_FIELD, send_early, 0)
     others = staged.at[pl.ds(1, FIELDS - 1)]
     pltpu.make_async_copy(others, others, stage_sem.at[2]).wait()
     lax.fori_loop(PER_FIELD, LAST * PER_FIELD, send_early, 0)
-    lax.fori_loop(0, PER_FIELD - 1, send_late, 0)
-    for i in range(LAST_PIECES):
-        first = ROWS - MAIN_ROWS + i * LAST_ROWS
-        send_piece(LAST + PER_FIELD - 1 + i, LAST, first, LAST_ROWS)
+    for k, (start, size) in enumerate(LATE):
+
+        def send_late(i, carry, k=k, start=start):
+            send_piece(LAST + k, LAST, start + i * PIECE_ROWS, PIECE_ROWS)
+            return carry
+
+        lax.fori_loop(0, size // PIECE_ROWS, send_late, 0)
 
     mask_copy.wait()
 
@@ -196,7 +205,7 @@
     old_copy.wait()
 
     def pack_piece(arrival, f, first, size):
-        piece = landed.at[f, :, pl.ds(pl.multiple_of(first, 8), size), :]
+        piece = landed.at[f, :, pl.ds(at_eight(first), size), :]
         pltpu.make_async_copy(piece, piece, recv_sem.at[arrival]).wait()
 
         def pack(k, squares):
@@ -206,14 +215,6 @@
 
     def pack_early(f, carry):
         pack_piece(f, f, 0, ROWS)
-        return carry
-
-    def pack_late(i, carry):
-        pack_piece(LAST + i, LAST, i * MAIN_ROWS, MAIN_ROWS)
-        return carry
-
-    def pack_last(i, carry):
-        pack_piece(LAST + PER_FIELD - 1 + i, LAST, ROWS - MAIN_ROWS + i * LAST_ROWS, LAST_ROWS)
         return carry
 
     pack_early(0, 0)
@@ -224,8 +225,8 @@
             pl.semaphore_signal(group_sem, inc=1, device_id=(s, b), device_id_type=MESH)
 
     lax.fori_loop(1, LAST, pack_early, 0)
-    lax.fori_loop(0, PER_FIELD - 1, pack_late, 0)
-    lax.fori_loop(0, LAST_PIECES, pack_last, 0)
+    for k, (start, size) in enumerate(LATE):
+        pack_piece(LAST + k, LAST, start, size)
 
     ocean = count[0]
     for g in range(1, GROUPS):
@@ -237,13 +238,12 @@
 
     pl.semaphore_wait(group_sem, 1)
     for dz, dy in FAR_FIRST:
-        to = lax.rem(io // 4 + dz, 4) * 4 + lax.rem(lax.rem(io, 4) + dy, 4)
         pltpu.make_async_remote_copy(
             src_ref=parts.at[io],
             dst_ref=parts.at[io],
             send_sem=part_send,
             recv_sem=part_recv,
-            device_id=(to, b),
+            device_id=(band_at(io, dz, dy), b),
             device_id_type=MESH,
         ).start()
 

time: 88.2 us -> 88.2 us (level)
  no operation moved by 1% of the time
where the time goes in v5:
time: 88.2 us; the launch traced here: 88.1 us
  Pallas kernels  87.4 us (99%)
    pallas_call x1, Pallas kernels, on_device(): pl.pallas_call(kernel, out_shape=(pltpu.VMEM(mean_old.shape, jnp.float32)...  85.2 us
    pallas_call x1, Pallas kernels, on_device(): pl.pallas_call(write, out_shape=(jax.ShapeDtypeStruct(mean_old.shape, jnp...  2.19 us

profile of v5, /device:TPU:0, one launch (start us, length us, event | category | flops | bytes accessed | tf_op | source)
XLA Modules:
  0.0 88.1 jit_solution(15511587324552142435)
XLA Ops:
  0.6 85.2 %shard_map.50 = (f32[6,1,64,3072]{3,2,1,0:T(8,128)S(1)}, f32[8,128]{1,0:T(8,128)S(1)}) custom-call(f32[6,8,128,256]{3,2,1,0:T(8,128)} %fields.1, f32[6,1,64,3072]{3,2,1,0:T(8,128)} %mean_old.1, s32[1,64,4096]{2,1,0:T(8,128)} %land_mask.1), custom_call_target="tpu_custom_call" | custom-call | tf_op jit(solution)/shard_map/pallas_call | solution.py:288
  85.9 2.2 %shard_map.51 = (f32[6,1,64,3072]{3,2,1,0:T(8,128)}, f32[1,6]{1,0:T(1,128)}) custom-call(f32[6,1,64,3072]{3,2,1,0:T(8,128)S(1)} %get-tuple-element.6.new, f32[8,128]{1,0:T(8,128)S(1)} %get-tuple-element.7.sums), custom_call_target="tpu_custom_call" | custom-call | tf_op jit(solution)/shard_map/pallas_call | solution.py:319

commit v6 on v4

--- a/solution.py
+++ b/solution.py
@@ -20,7 +20,7 @@
 PER_FIELD = ROWS // MAIN_ROWS
 LAST_PIECES = MAIN_ROWS // LAST_ROWS
 ARRIVALS = LAST + PER_FIELD - 1 + LAST_PIECES
-ORDER = [(dx, dy, dc) for dc in (0, 1) for dx in (2, 1, 3, 0) for dy in (0, 1)]
+ORDER = [(dx, dy, dc) for dc in (0, 1) for dx in (1, 3, 2, 0) for dy in (0, 1)]
 
 
 RING_HOPS = (0, 1, 2, 1)
@@ -28,6 +28,10 @@
     ((dz, dy) for dz in range(4) for dy in range(4) if (dz, dy) != (0, 0)),
     key=lambda d: -RING_HOPS[d[0]] - RING_HOPS[d[1]],
 )
+
+
+def band_at(io, dz, dy):
+    return lax.rem(io // 4 + dz, 4) * 4 + lax.rem(lax.rem(io, 4) + dy, 4)
 
 
 def lanes_of(array, index):
@@ -108,8 +112,10 @@
     keeps = (io // 2) == b
 
     barrier = pltpu.get_barrier_semaphore()
-    for s in range(LON):
-        pl.semaphore_signal(barrier, inc=1, device_id=(s, io // 2), device_id_type=MESH)
+    for dz, dy in FAR_FIRST + [(0, 0)]:
+        pl.semaphore_signal(
+            barrier, inc=1, device_id=(band_at(io, dz, dy), io // 2), device_id_type=MESH
+        )
     def stage(f, first, size, sem):
         return [
             pltpu.make_async_copy(
@@ -237,13 +243,12 @@
 
     pl.semaphore_wait(group_sem, 1)
     for dz, dy in FAR_FIRST:
-        to = lax.rem(io // 4 + dz, 4) * 4 + lax.rem(lax.rem(io, 4) + dy, 4)
         pltpu.make_async_remote_copy(
             src_ref=parts.at[io],
             dst_ref=parts.at[io],
             send_sem=part_send,
             recv_sem=part_recv,
-            device_id=(to, b),
+            device_id=(band_at(io, dz, dy), b),
             device_id_type=MESH,
         ).start()
 

time: 88.2 us -> 88.2 us (level)
  no operation moved by 1% of the time
where the time goes in v6:
time: 88.2 us; the launch traced here: 88.1 us
  Pallas kernels  87.5 us (99%)
    pallas_call x1, Pallas kernels, on_device(): pl.pallas_call(kernel, out_shape=(pltpu.VMEM(mean_old.shape, jnp.float32)...  85.3 us
    pallas_call x1, Pallas kernels, on_device(): pl.pallas_call(write, out_shape=(jax.ShapeDtypeStruct(mean_old.shape, jnp...  2.19 us

profile of v6, /device:TPU:0, one launch (start us, length us, event | category | flops | bytes accessed | tf_op | source)
XLA Modules:
  0.0 88.1 jit_solution(12468346982025665554)
XLA Ops:
  0.6 85.3 %shard_map.50 = (f32[6,1,64,3072]{3,2,1,0:T(8,128)S(1)}, f32[8,128]{1,0:T(8,128)S(1)}) custom-call(f32[6,8,128,256]{3,2,1,0:T(8,128)} %fields.1, f32[6,1,64,3072]{3,2,1,0:T(8,128)} %mean_old.1, s32[1,64,4096]{2,1,0:T(8,128)} %land_mask.1), custom_call_target="tpu_custom_call" | custom-call | tf_op jit(solution)/shard_map/pallas_call | solution.py:293
  85.9 2.2 %shard_map.51 = (f32[6,1,64,3072]{3,2,1,0:T(8,128)}, f32[1,6]{1,0:T(1,128)}) custom-call(f32[6,1,64,3072]{3,2,1,0:T(8,128)S(1)} %get-tuple-element.6.new, f32[8,128]{1,0:T(8,128)S(1)} %get-tuple-element.7.sums), custom_call_target="tpu_custom_call" | custom-call | tf_op jit(solution)/shard_map/pallas_call | solution.py:324
